TPU v7x, 512 devices: a whole 4x8x8 slice. The times are simulated.
512 devices in a mesh: batch: 32 (over z, x), head: 16 (over y, core).
Axes of the slice: x: 4, y: 8, z: 8, core: 2. Of those that a mesh axis runs over, the one named last changes fastest.
Arguments:
- tokens: bfloat16 [16384, 2048], P('batch', 'head'), may hold values from -96 to 96
- lengths: int32 [128], P('batch'), may hold values from 1 to 128
- states: float32 [128, 16, 128, 128], P('batch', 'head'), may hold values from -3 to 3
- norm_gain: float32 [2048], replicated, may hold values from 0.1 to 1.9
- mix_weight: bfloat16 [2048, 14336], P(None, 'head'), may hold values from -0.125 to 0.125
- rate_weight: bfloat16 [2048, 64], P(None, 'head'), may hold values from -0.5524272 to 0.5524272
- decay_rate: float32 [16], P('head'), may hold values from 0.0005 to 0.03
- head_gain: float32 [128], replicated, may hold values from 0.1 to 1.9
- out_weight: bfloat16 [2048, 2048], P('head'), may hold values from -0.125 to 0.125
- final_gain: float32 [2048], replicated, may hold values from 0.1 to 1.9
- vocab_table: bfloat16 [16384, 2048], P(('batch', 'head')), may hold values from -50.8233 to 50.8233
- next_token: int32 [128], replicated, may hold values from 0 to 16383
Outputs:
- mixed: bfloat16 [16384, 2048], P('batch', 'head')
- new_state: float32 [128, 16, 128, 128], P('batch', 'head')
- log_likelihood: float32 [128], replicated
All inputs are finite; a program needn't handle non-finite values.
Results may differ from a plain program's by a relative error of at most 0.0058.
The roundings to bfloat16 on the way count: a program that leaves them out, or rounds other values in their place, can miss the bound.
Values may be sent and summed in bfloat16 or wider, within the bound.
A program may use at most 64 MiB of HBM per device.

v0:
```python
import jax
import jax.numpy as jnp
from jax import lax
from jax.sharding import Mesh
from jax.sharding import PartitionSpec as P

HEAD_DIM = 128
REFLECT = 3
NEW_POSITIONS = 128
HEAD = ("head_0", "head_1")
BATCH_HEAD = ("batch_0", "batch_1", "head_0", "head_1")
BATCH = ("batch_0", "batch_1")
ROW_EPSILON = 1e-05
KEY_EPSILON = 1e-06
HIGHEST_PRECISION = lax.Precision.HIGHEST


def all_in_one(array, axis):
    leaves = jax.tree.leaves(array)
    order = sorted(range(len(leaves)), key=lambda k: -leaves[k].size)
    width = (1, *leaves[order[0]].shape)[-1]
    lines = [
        jnp.pad(leaves[k].reshape(-1), (0, -leaves[k].size % width)).reshape(-1, width)
        for k in order
    ]
    both, at, found = (lax.all_gather(jnp.concatenate(lines), axis), 0, {})
    for k, line in zip(order, lines):
        share = both[:, at : at + len(line)].reshape(len(both), -1)
        found[k] = share[:, : leaves[k].size].reshape(-1, *leaves[k].shape)
        at += len(line)
    numbers = iter(range(len(leaves)))
    return jax.tree.map(lambda _: found[next(numbers)], array)


def joined_all(array, axes, combine):
    for axis in axes:
        pieces = all_in_one(array, axis)
        array = jax.tree.map(lambda part: part[0], pieces)
        for k in range(1, lax.axis_size(axis)):
            array = combine(array, jax.tree.map(lambda part: part[k], pieces))
    return array


def delta_block(queries, key_rows, value_rows, beta_rows, log_decay, start_state):
    positions = key_rows.shape[0]
    reflections = key_rows.shape[1]
    total_steps = positions * reflections
    flat_keys = key_rows.reshape(total_steps, key_rows.shape[2])
    flat_values = value_rows.reshape(total_steps, value_rows.shape[2])
    flat_betas = beta_rows.reshape(total_steps)
    padding = jnp.zeros((positions, reflections - 1), log_decay.dtype)
    step_decay = jnp.concatenate([log_decay[:, None], padding], axis=1).reshape(total_steps)
    cumulative = jnp.cumsum(step_decay)
    step_index = jnp.arange(total_steps)
    earlier = step_index[:, None] > step_index[None, :]
    decay_ratio = jnp.exp(jnp.where(earlier, cumulative[:, None] - cumulative[None, :], -jnp.inf))
    key_gram = jnp.dot(flat_keys, flat_keys.T, precision=HIGHEST_PRECISION)
    system = (
        jnp.eye(total_steps, dtype=key_gram.dtype) + flat_betas[:, None] * decay_ratio * key_gram
    )
    start_image = jnp.dot(flat_keys, start_state.T, precision=HIGHEST_PRECISION)
    source = flat_betas[:, None] * (flat_values - jnp.exp(cumulative)[:, None] * start_image)
    updates = jax.scipy.linalg.solve_triangular(system, source, lower=True, unit_diagonal=True)
    query_cumulative = cumulative.reshape(positions, reflections)[:, reflections - 1]
    query_step = step_index.reshape(positions, reflections)[:, reflections - 1]
    visible = step_index[None, :] <= query_step[:, None]
    weights = jnp.exp(jnp.where(visible, query_cumulative[:, None] - cumulative[None, :], -jnp.inf))
    scores = jnp.dot(queries, flat_keys.T, precision=HIGHEST_PRECISION) * weights
    attended = jnp.exp(query_cumulative)[:, None] * jnp.dot(
        queries, start_state.T, precision=HIGHEST_PRECISION
    )
    attended = attended + jnp.dot(scores, updates, precision=HIGHEST_PRECISION)
    tail_decay = jnp.exp(cumulative[total_steps - 1] - cumulative)
    new_state = jnp.exp(cumulative[total_steps - 1]) * start_state
    new_state = new_state + jnp.dot(
        updates.T, tail_decay[:, None] * flat_keys, precision=HIGHEST_PRECISION
    )
    return (attended, new_state)


def head_inputs(projected, rate_logits, valid_mask, decay_rate):
    queries = jax.nn.silu(projected[:, :, :, 0])
    key_rows = jax.nn.silu(projected[:, :, :, 1 : REFLECT + 1])
    key_rows = key_rows * lax.rsqrt(
        jnp.sum(key_rows * key_rows, axis=-1, keepdims=True) + KEY_EPSILON
    )
    value_rows = jax.nn.silu(projected[:, :, :, REFLECT + 1 :])
    beta_rows = jnp.where(
        valid_mask[:, :, None, None], 2.0 * jax.nn.sigmoid(rate_logits[..., :REFLECT]), 0.0
    )
    log_decay = jnp.where(
        valid_mask[:, :, None], -decay_rate * jax.nn.softplus(rate_logits[..., REFLECT]), 0.0
    )
    return (queries, key_rows, value_rows, beta_rows, log_decay)


def run_heads(queries, key_rows, value_rows, beta_rows, log_decay, start_states):
    per_head = jax.vmap(delta_block, in_axes=(1, 1, 1, 1, 1, 0), out_axes=(1, 0))
    per_sequence = jax.vmap(per_head)
    return per_sequence(queries, key_rows, value_rows, beta_rows, log_decay, start_states)


def head_norm(attended, head_gain):
    factor = lax.rsqrt(jnp.mean(attended * attended, axis=-1, keepdims=True) + ROW_EPSILON)
    return (attended * factor * head_gain).astype(jnp.bfloat16)


def combine_totals(earlier_part, later_part):
    highest = jnp.maximum(earlier_part[0], later_part[0])
    summed = earlier_part[1] * jnp.exp(earlier_part[0] - highest) + later_part[1] * jnp.exp(
        later_part[0] - highest
    )
    return (highest, summed, earlier_part[2] + later_part[2])


def on_device(
    tokens,
    lengths,
    states,
    norm_gain,
    mix_weight,
    rate_weight,
    decay_rate,
    head_gain,
    out_weight,
    final_gain,
    vocab_table,
    next_token,
):
    sequences = lengths.shape[0]
    local_rows = tokens.shape[0]
    local_width = tokens.shape[1]
    model_width = norm_gain.shape[0]
    local_heads = states.shape[1]
    wide_portion = lax.all_gather(tokens, HEAD, axis=1, tiled=True).astype(jnp.float32)
    scaled = (wide_portion * norm_gain).astype(jnp.bfloat16)
    projected = jnp.dot(scaled, mix_weight, preferred_element_type=jnp.float32)
    rate_logits = jnp.dot(scaled, rate_weight, preferred_element_type=jnp.float32)
    squares = jnp.sum(wide_portion * wide_portion, axis=1)
    projected, rate_logits, squares = (projected, rate_logits, squares)
    inverse = lax.rsqrt(squares / model_width + ROW_EPSILON)
    projected = (projected * inverse[:, None]).reshape(
        sequences, NEW_POSITIONS, local_heads, 2 * REFLECT + 1, HEAD_DIM
    )
    rate_logits = (rate_logits * inverse[:, None]).reshape(
        sequences, NEW_POSITIONS, local_heads, REFLECT + 1
    )
    valid_mask = jnp.arange(NEW_POSITIONS)[None, :] < lengths[:, None]
    queries, key_rows, value_rows, beta_rows, log_decay = head_inputs(
        projected, rate_logits, valid_mask, decay_rate
    )
    attended, new_state = run_heads(queries, key_rows, value_rows, beta_rows, log_decay, states)
    normed = head_norm(attended, head_gain).reshape(local_rows, local_heads * HEAD_DIM)
    columns = lax.all_to_all(out_weight, HEAD, split_axis=1, concat_axis=0, tiled=True)
    mix_sum = jnp.dot(
        lax.all_gather(normed, HEAD, axis=1, tiled=True),
        columns,
        preferred_element_type=jnp.float32,
    )
    mixed = (tokens.astype(jnp.float32) + mix_sum).astype(jnp.bfloat16)
    last_index = (lengths - 1)[:, None, None]
    last_rows = jnp.take_along_axis(
        mixed.reshape(sequences, NEW_POSITIONS, local_width), last_index, axis=1
    )[:, 0]
    gathered = lax.all_gather(last_rows[None], BATCH_HEAD, axis=0, tiled=True)
    batch_count = lax.axis_size(BATCH)
    head_count = lax.axis_size(HEAD)
    everyone = gathered.reshape(batch_count, head_count, sequences, local_width).transpose(
        0, 2, 1, 3
    )
    everyone = everyone.reshape(batch_count * sequences, model_width)
    widened_all = everyone.astype(jnp.float32)
    factor = lax.rsqrt(jnp.mean(widened_all * widened_all, axis=1, keepdims=True) + ROW_EPSILON)
    hidden = (widened_all * factor * final_gain).astype(jnp.bfloat16)
    logits = jnp.dot(hidden, vocab_table.T, preferred_element_type=jnp.float32)
    vocab_here = vocab_table.shape[0]
    vocab_ids = lax.axis_index(BATCH_HEAD) * vocab_here + jnp.arange(vocab_here)
    largest = jnp.max(logits, axis=1)
    exp_total = jnp.sum(jnp.exp(logits - largest[:, None]), axis=1)
    target = jnp.sum(jnp.where(vocab_ids[None, :] == next_token[:, None], logits, 0.0), axis=1)
    largest, exp_total, target = joined_all(
        (largest, exp_total, target), BATCH_HEAD, combine_totals
    )
    return (mixed, new_state, target - (largest + jnp.log(exp_total)))


def solution(mesh):
    torus = Mesh(mesh.devices.reshape(8, 4, 8, 2), ("batch_0", "batch_1", "head_0", "head_1"))
    placed = (
        P(BATCH, HEAD),
        P(BATCH),
        P(BATCH, HEAD, None, None),
        P(),
        P(None, HEAD),
        P(None, HEAD),
        P(HEAD),
        P(),
        P(HEAD, None),
        P(),
        P(BATCH_HEAD, None),
        P(),
    )
    return jax.shard_map(
        on_device,
        mesh=torus,
        in_specs=placed,
        out_specs=(P(BATCH, HEAD), P(BATCH, HEAD, None, None), P()),
        check_vma=False,
    )
```

profile of v0, /device:TPU:1, one launch (start us, length us, event | category | flops | bytes accessed | tf_op | source)
XLA Modules:
  0.0 411.4 jit_solution(3345442622129094462)
XLA Ops:
  7.2 0.7 all-gather.11.cloned.1.call-update
  8.6 0.6 iota_multiply_fusion
  9.2 1.1 fusion.28
  10.4 1.2 iota_compare_fusion.5
  11.6 0.7 iota_compare_fusion.4
  12.3 0.9 iota_compare_fusion.1
  13.2 45.9 %all-gather.11.cloned.1.call-done = bf16[512,2048]{1,0:T(8,128)(2,1)} async-done(((bf16[512,128]{1,0:T(8,128)(2,1)}), bf16[512,2048]{1,0:T(8,128)(2,1)}) %all-gather.11.cloned.1.call-update) | async-done | bytes 2097168 | tf_op jit(solution)/shard_map/all_gather | solution.py:135
  59.1 2.1 fusion.1
  61.2 2.4 fusion.19
  64.1 1.2 reduce-window.6
  65.3 0.7 slice.491
  66.2 5.6 %fusion.6 = f32[512,896]{1,0:T(8,128)} fusion(bf16[2048,896]{1,0:T(8,128)(2,1)} %param.16, bf16[512,2048]{1,0:T(8,128)(2,1)S(1)} %copy-done.1, f32[2048]{0:T(1024)S(1)} %copy-done.21, f32[512]{0:T(512)S(1)} %add_rsqrt_fusion.2), kind=kOutput, calls=%fused_computation.10 | convolution fusion | flops 1882652672 | bytes 7612416 | tf_op jit(solution)/shard_map/dot_general | solution.py:137
  71.8 1.6 reshape.1914
  73.4 0.9 slice.495
  74.3 1.4 fusion.132
  75.7 0.8 copy.214
  76.9 1.7 divide_multiply_fusion
  81.3 5.3 %select_add_fusion = f32[4,384,384]{2,1,0:T(8,128)} fusion(f32[384,384]{1,0:T(8,128)} %get-tuple-element.100, f32[4,384]{1,0:T(4,128)S(1)} %get-tuple-element.86, f32[4,384]{1,0:T(4,128)S(1)} %mul.576, f32[384,384]{1,0:T(8,128)} %get-tuple-element.99, pred[384,384]{1,0:T(8,128)(4,1)S(1)} %copy-done.7, pred[384,384]{1,0:T(8,128)(4,1)S(1)} %copy-done.8, ...), kind=kOutput, calls=%fused_computation.7 | convolution fusion | flops 910098432 | bytes 4632576 | tf_op jit(solution)/shard_map/vmap(vmap())/dot_general | solution.py:57
  86.6 11.4 %while.1 = (s32[]{:T(128)}, f32[4,1,384,384]{3,2,1,0:T(8,128)}, s32[3,2]{0,1:T(2,128)S(1)}, f32[3,4,1,128,128]{4,3,0,2,1:T(8,128)}, s32[]{:T(128)}) while((s32[]{:T(128)}, f32[4,1,384,384]{3,2,1,0:T(8,128)}, s32[3,2]{0,1:T(2,128)S(1)}, f32[3,4,1,128,128]{4,3,0,2,1:T(8,128)}, s32[]{:T(128)}) %tuple.58), condition=%wide.while_cond, body=%wide.while_body.sunk | while | flops 2 | bytes 525421 | solution.py:63
  86.7 0.6 fusion.144
  87.2 3.2 bitcast_dynamic-update-slice_fusion.2
  91.0 3.2 bitcast_dynamic-update-slice_fusion.2
  94.9 3.1 bitcast_dynamic-update-slice_fusion.2
  98.0 118.9 %custom-call.4 = f32[4,1,3,128,128]{3,4,2,1,0:T(8,128)S(1)} custom-call(f32[4,1,3,128,128]{4,3,2,1,0:T(8,128)} %bitcast.624), custom_call_target="InvertDiagBlocksLowerTriangular" | custom-call | tf_op jit(solution)/shard_map/vmap(vmap(jit(_solve_triangular)))/triangular_solve | solution.py:63
  216.9 0.9 fusion.11
  217.8 0.6 fusion.34
  218.4 1.4 fusion.13
  219.8 0.6 convolution_bitcast_fusion.2
  220.4 1.7 fusion.15
  222.1 0.6 convolution_bitcast_fusion
  223.1 0.7 convolution_multiply_fusion.2
  223.9 1.1 convolution_multiply_fusion.1
  224.9 1.0 multiply_reduce_fusion.2
  225.9 0.8 fusion.36
  226.8 1.0 copy.235
  227.8 5.1 %all-to-all-start = ((bf16[128,16,128]{0,2,1:T(8,128)(2,1)}), bf16[128,16,128]{0,2,1:T(8,128)(2,1)S(1)}, u32[]{:S(2)}, u32[]{:S(2)}) async-start(bf16[128,16,128]{0,2,1:T(8,128)(2,1)} %bitcast.33), calls=%async_computation | async-start | bytes 1048576 | tf_op jit(solution)/shard_map/all_to_all | solution.py:154
  233.0 18.5 %all-to-all-done = bf16[128,16,128]{0,2,1:T(8,128)(2,1)S(1)} async-done(((bf16[128,16,128]{0,2,1:T(8,128)(2,1)}), bf16[128,16,128]{0,2,1:T(8,128)(2,1)S(1)}, u32[]{:S(2)}, u32[]{:S(2)}) %all-to-all-start) | async-done | bytes 524320 | tf_op jit(solution)/shard_map/all_to_all | solution.py:154
  251.8 0.7 exp.430
  253.1 2.1 fusion.17
  255.3 18.9 %all-gather.13.cloned.1.call-done = bf16[512,2048]{1,0:T(8,128)(2,1)} async-done(((bf16[512,128]{1,0:T(8,128)(2,1)}), bf16[512,2048]{1,0:T(8,128)(2,1)}) %all-gather.13.cloned.1.call-update) | async-done | bytes 2097168 | tf_op jit(solution)/shard_map/all_gather | solution.py:156
  274.2 2.3 fusion.18
  276.5 0.6 gather_fusion
  277.2 70.2 %all_gather.35 = bf16[512,4,128]{2,1,0:T(4,128)(2,1)S(1)} all-gather(bf16[1,4,128]{2,1,0:T(4,128)(2,1)S(1)} %bitcast_select_fusion), channel_id=1, replica_groups=mesh['batch_0'=8,'batch_1'=4,'head_0'=8,'head_1'=2] {'batch_0','batch_1'..., dimensions={0}, use_global_device_ids=true | all-gather | bytes 525312 | tf_op jit(solution)/shard_map/all_gather | solution.py:165
  347.4 0.6 multiply_reduce_fusion
  348.9 15.8 %all-gather.4 = f32[8,3,128]{2,1,0:T(4,128)S(1)} all-gather(f32[1,3,128]{2,1,0:T(4,128)S(1)} %maximum_bitcast_fusion.5), channel_id=2, replica_groups=mesh['batch_0'=8,'batch_1'=4,'head_0'=8,'head_1'=2] {'batch_0'}, dimensions={0}, use_global_device_ids=true | all-gather | bytes 13824 | tf_op jit(solution)/shard_map/all_gather | solution.py:26
  364.8 8.1 %all-gather.5 = f32[4,3,128]{2,1,0:T(4,128)S(1)} all-gather(f32[1,3,128]{2,1,0:T(4,128)S(1)} %maximum_bitcast_fusion.6), channel_id=3, replica_groups=mesh['batch_0'=8,'batch_1'=4,'head_0'=8,'head_1'=2] {'batch_1'}, dimensions={0}, use_global_device_ids=true | all-gather | bytes 7680 | tf_op jit(solution)/shard_map/all_gather | solution.py:26
  373.0 15.6 %all-gather.6 = f32[8,3,128]{2,1,0:T(4,128)S(1)} all-gather(f32[1,3,128]{2,1,0:T(4,128)S(1)} %maximum_bitcast_fusion.7), channel_id=4, replica_groups=mesh['batch_0'=8,'batch_1'=4,'head_0'=8,'head_1'=2] {'head_0'}, dimensions={0}, use_global_device_ids=true | all-gather | bytes 13824 | tf_op jit(solution)/shard_map/all_gather | solution.py:26
  388.6 15.4 %all-gather.7 = f32[2,3,128]{2,1,0:T(4,128)S(1)} all-gather(f32[1,3,128]{2,1,0:T(4,128)S(1)} %maximum_bitcast_fusion.8), channel_id=5, replica_groups=mesh['batch_0'=8,'batch_1'=4,'head_0'=8,'head_1'=2] {'head_1'}, dimensions={0}, use_global_device_ids=true | all-gather | bytes 4608 | tf_op jit(solution)/shard_map/all_gather | solution.py:26
  (115 shorter events, 8.1 us)
Async XLA Ops:
  7.2 341.1 %copy-start = (bf16[32,2048]{1,0:T(8,128)(2,1)S(1)}, bf16[32,2048]{1,0:T(8,128)(2,1)}, u32[]{:S(2)}) copy-start(bf16[32,2048]{1,0:T(8,128)(2,1)} %param.22) | copy-start | bytes 393220
  7.2 54.0 %copy-start.20 = (bf16[2048,4]{0,1:T(4,128)(2,1)S(1)}, bf16[2048,4]{0,1:T(4,128)(2,1)}, u32[]{:S(2)}) copy-start(bf16[2048,4]{0,1:T(4,128)(2,1)} %param.17) | copy-start | bytes 49156
  7.2 54.0 %copy-start.21 = (f32[2048]{0:T(1024)S(1)}, f32[2048]{0:T(1024)}, u32[]{:S(2)}) copy-start(f32[2048]{0:T(1024)} %param.15) | copy-start | bytes 24580
  7.2 51.9 %all-gather.11.cloned.1.call-start = ((), (), s32[]{:S(2)}) async-start(), calls=%async_computation.1 | async-start | bytes 2228224 | tf_op jit(solution)/shard_map/all_gather | solution.py:135
  7.9 266.2 %all-gather.13.cloned.1.call-start = ((), (), s32[]{:S(2)}) async-start(), calls=%async_computation.2 | async-start | bytes 2228224 | tf_op jit(solution)/shard_map/all_gather | solution.py:156
  13.2 50.4 %copy-start.17 = (s32[4]{0:T(128)S(1)}, s32[4]{0:T(128)}, u32[]{:S(2)}) copy-start(s32[4]{0:T(128)} %param.13) | copy-start | bytes 52
  61.2 5.0 %copy-start.1 = (bf16[512,2048]{1,0:T(8,128)(2,1)S(1)}, bf16[512,2048]{1,0:T(8,128)(2,1)}, u32[]{:S(2)}) copy-start(bf16[512,2048]{1,0:T(8,128)(2,1)} %all-gather.11.cloned.1.call-done) | copy-start | bytes 6291460
  63.6 13.0 %copy-start.10 = (f32[4,128,1,4]{1,0,3,2:T(4,128)}, f32[4,128,1,4]{1,0,3,2:T(4,128)S(1)}, u32[]{:S(2)}) copy-start(f32[4,128,1,4]{1,0,3,2:T(4,128)S(1)} %reshape.1828) | copy-start | bytes 24580
  78.6 0.9 slice-start
  78.6 1.1 copy-start.16
  78.9 2.4 copy-start.7
  78.9 2.3 copy-start.8
  80.7 0.5 copy-start.14
  81.2 5.3 %copy-start.11 = (f32[4,384]{1,0:T(4,128)}, f32[4,384]{1,0:T(4,128)S(1)}, u32[]{:S(2)}) copy-start(f32[4,384]{1,0:T(4,128)S(1)} %get-tuple-element.86) | copy-start | bytes 18436
  81.3 5.3 %copy-start.22 = (s32[3]{0:T(128)S(1)}, s32[3]{0:T(128)}, u32[]{:S(2)}) copy-start(s32[3]{0:T(128)} %iota_multiply_fusion) | copy-start | bytes 40
  86.6 130.3 %copy-start.2 = (f32[4,1,128,128]{3,2,1,0:T(8,128)S(1)}, f32[4,1,128,128]{3,2,1,0:T(8,128)}, u32[]{:S(2)}) copy-start(f32[4,1,128,128]{3,2,1,0:T(8,128)} %param.14) | copy-start | bytes 786436
  218.4 4.7 %copy-start.5 = (f32[4,128,1,1,128]{4,3,1,0,2:T(1,128)S(1)}, f32[4,128,1,1,128]{4,3,1,0,2:T(1,128)}, u32[]{:S(2)}) copy-start(f32[4,128,1,1,128]{4,3,1,0,2:T(1,128)} %slice.495) | copy-start | bytes 786436
  219.8 4.0 copy-start.9
  219.8 4.0 copy-start.12
  223.8 2.1 copy-start.15
  223.8 2.9 copy-start.4
  225.9 7.0 %copy-start.18 = (s32[4]{0:T(128)S(1)}, s32[4]{0:T(128)}, u32[]{:S(2)}) copy-start(s32[4]{0:T(128)} %param.13) | copy-start | bytes 52
  227.8 23.8 %all-to-all-start = ((bf16[128,16,128]{0,2,1:T(8,128)(2,1)}), bf16[128,16,128]{0,2,1:T(8,128)(2,1)S(1)}, u32[]{:S(2)}, u32[]{:S(2)}) async-start(bf16[128,16,128]{0,2,1:T(8,128)(2,1)} %bitcast.33), calls=%async_computation | async-start | bytes 1048576 | tf_op jit(solution)/shard_map/all_to_all | solution.py:154
  251.5 22.6 %copy-start.3 = (bf16[512,128]{1,0:T(8,128)(2,1)S(1)}, bf16[512,128]{1,0:T(8,128)(2,1)}, u32[]{:S(2)}) copy-start(bf16[512,128]{1,0:T(8,128)(2,1)} %param.12) | copy-start | bytes 393220
  274.2 74.1 %copy-start.13 = (f32[2048]{0:T(1024)S(1)}, f32[2048]{0:T(1024)}, u32[]{:S(2)}) copy-start(f32[2048]{0:T(1024)} %param.21) | copy-start | bytes 24580
  276.5 128.1 %copy-start.6 = (bf16[512,128]{1,0:T(8,128)(2,1)}, bf16[512,128]{1,0:T(8,128)(2,1)S(1)}, u32[]{:S(2)}) copy-start(bf16[512,128]{1,0:T(8,128)(2,1)S(1)} %fusion.18) | copy-start | bytes 393220
  276.5 72.3 %copy-start.19 = (s32[128]{0:T(128)S(1)}, s32[128]{0:T(128)}, u32[]{:S(2)}) copy-start(s32[128]{0:T(128)} %param.23) | copy-start | bytes 1540
Sparse Core Ops, SparseCore 0:
  10.1 48.9 all-gather.10
  226.9 47.2 all-gather.12
where the time goes:
time: 412 us; the launch traced here: 411 us
  other arithmetic  132 us (32%)
  blocking collectives  125 us (30%)
  waiting for transfers between devices  84 us (20%)
  matrix products  26.7 us (6%)
  local copies, waits for them, and re-layouts  22.6 us (5%)
  between operations  15.3 us (4%)
  starting transfers between devices  5.22 us (1%)
    another operation x3, other arithmetic, delta_block(): jax.scipy.linalg.solve_triangular(system, source, lower=True, unit_diagon...  119 us
    all_gather x1, blocking collectives, on_device(): gathered = lax.all_gather(last_rows[None], BATCH_HEAD, axis=0, tiled=True)  70.2 us
    all_gather x4, blocking collectives, all_in_one(): both, at, found = (lax.all_gather(jnp.concatenate(lines), axis), 0, {})  55 us
    all_gather x1, waiting for transfers between devices, on_device(): lax.all_gather(tokens, HEAD, axis=1, tiled=True).astype(jnp.float32)  45.9 us
    all_gather x1, waiting for transfers between devices, on_device(): lax.all_gather(normed, HEAD, axis=1, tiled=True)  18.9 us
    all_to_all x1, waiting for transfers between devices, on_device(): lax.all_to_all(out_weight, HEAD, split_axis=1, concat_axis=0, tiled=True)  18.5 us
    another operation x20, local copies, waits for them, and re-layouts  13.7 us
  transfers between devices with their start and end apart: 3, of which 3 were waited for; matrix products, arithmetic and copies ran while one was open for 2% of the time, Pallas kernels for 0%

commit v1 on v0

--- a/solution.py
+++ b/solution.py
@@ -162,7 +162,11 @@
     last_rows = jnp.take_along_axis(
         mixed.reshape(sequences, NEW_POSITIONS, local_width), last_index, axis=1
     )[:, 0]
-    gathered = lax.all_gather(last_rows[None], BATCH_HEAD, axis=0, tiled=True)
+    x_part = last_rows[None]
+    by_rank = []
+    for _ in range(lax.axis_size(BATCH_HEAD)):
+        by_rank.append(x_part)
+    gathered = jnp.concatenate(lax.all_to_all(jnp.stack(by_rank), BATCH_HEAD, 0, 0), axis=0)
     batch_count = lax.axis_size(BATCH)
     head_count = lax.axis_size(HEAD)
     everyone = gathered.reshape(batch_count, head_count, sequences, local_width).transpose(

time: 412 us -> 380 us (0.922)
  blocking collectives: 125 us -> 54 us
  waiting for transfers between devices: 84 us -> 106 us
  starting transfers between devices: 5.22 us -> 20.7 us
    all_gather x1 -> x0, blocking collectives: 70.2 us -> none  [on_device(): gathered = lax.all_gather(last_rows[None], BATCH_HEAD, axis=0, tiled=True)]
    all_to_all x0 -> x1, waiting for transfers between devices: none -> 19.9 us  [on_device(): lax.all_to_all(jnp.stack(by_rank), BATCH_HEAD, 0, 0)]
    all_to_all x0 -> x1, starting transfers between devices: none -> 15.5 us  [on_device(): lax.all_to_all(jnp.stack(by_rank), BATCH_HEAD, 0, 0)]
    another operation x20 -> x21, local copies, waits for them, and re-layouts: 13.7 us -> 14.5 us
  transfers between devices with their start and end apart: 3 -> 4, of which waited for: 3 -> 4; matrix products, arithmetic and copies ran while one was open for 2% -> 3% of each run, Pallas kernels for 0% -> 0%
where the time goes in v1:
time: 380 us; the launch traced here: 379 us
  other arithmetic  132 us (35%)
  waiting for transfers between devices  106 us (28%)
  blocking collectives  54 us (14%)
  matrix products  26.7 us (7%)
  local copies, waits for them, and re-layouts  24 us (6%)
  starting transfers between devices  20.7 us (5%)
  between operations  15.3 us (4%)
    another operation x3, other arithmetic, delta_block(): jax.scipy.linalg.solve_triangular(system, source, lower=True, unit_diagon...  119 us
    all_gather x4, blocking collectives, all_in_one(): both, at, found = (lax.all_gather(jnp.concatenate(lines), axis), 0, {})  54 us
    all_gather x1, waiting for transfers between devices, on_device(): lax.all_gather(tokens, HEAD, axis=1, tiled=True).astype(jnp.float32)  45.8 us
    all_gather x1, waiting for transfers between devices, on_device(): lax.all_gather(normed, HEAD, axis=1, tiled=True)  20.5 us
    all_to_all x1, waiting for transfers between devices, on_device(): lax.all_to_all(jnp.stack(by_rank), BATCH_HEAD, 0, 0)  19.9 us
    all_to_all x1, waiting for transfers between devices, on_device(): lax.all_to_all(out_weight, HEAD, split_axis=1, concat_axis=0, tiled=True)  19 us
    all_to_all x1, starting transfers between devices, on_device(): lax.all_to_all(jnp.stack(by_rank), BATCH_HEAD, 0, 0)  15.5 us
    another operation x20, local copies, waits for them, and re-layouts  13.6 us
  transfers between devices with their start and end apart: 4, of which 4 were waited for; matrix products, arithmetic and copies ran while one was open for 3% of the time, Pallas kernels for 0%

profile of v1, /device:TPU:1, one launch (start us, length us, event | category | flops | bytes accessed | tf_op | source)
XLA Modules:
  0.0 378.9 jit_solution(9148590202398283064)
XLA Ops:
  7.2 0.7 all-gather.11.cloned.1.call-update
  8.6 0.6 iota_multiply_fusion
  9.2 1.1 fusion.28
  10.4 1.3 iota_compare_fusion.5
  11.7 0.7 iota_compare_fusion.4
  12.4 0.9 iota_compare_fusion.1
  13.2 45.8 %all-gather.11.cloned.1.call-done = bf16[512,2048]{1,0:T(8,128)(2,1)} async-done(((bf16[512,128]{1,0:T(8,128)(2,1)}), bf16[512,2048]{1,0:T(8,128)(2,1)}) %all-gather.11.cloned.1.call-update) | async-done | bytes 2097168 | tf_op jit(solution)/shard_map/all_gather | solution.py:135
  59.1 2.1 fusion.1
  61.2 2.4 fusion.19
  64.1 1.2 reduce-window.6
  65.3 0.7 slice.491
  66.2 5.6 %fusion.6 = f32[512,896]{1,0:T(8,128)} fusion(bf16[2048,896]{1,0:T(8,128)(2,1)} %param.16, bf16[512,2048]{1,0:T(8,128)(2,1)S(1)} %copy-done.1, f32[2048]{0:T(1024)S(1)} %copy-done.21, f32[512]{0:T(512)S(1)} %add_rsqrt_fusion.2), kind=kOutput, calls=%fused_computation.10 | convolution fusion | flops 1882652672 | bytes 7612416 | tf_op jit(solution)/shard_map/dot_general | solution.py:137
  71.8 1.6 reshape.1905
  73.4 0.9 slice.495
  74.3 1.4 fusion.132
  75.8 0.8 copy.181
  77.0 1.7 divide_multiply_fusion
  81.3 5.3 %select_add_fusion = f32[4,384,384]{2,1,0:T(8,128)} fusion(f32[384,384]{1,0:T(8,128)} %get-tuple-element.93, f32[4,384]{1,0:T(4,128)S(1)} %get-tuple-element.79, f32[4,384]{1,0:T(4,128)S(1)} %mul.576, f32[384,384]{1,0:T(8,128)} %get-tuple-element.92, pred[384,384]{1,0:T(8,128)(4,1)S(1)} %copy-done.6, pred[384,384]{1,0:T(8,128)(4,1)S(1)} %copy-done.7, ...), kind=kOutput, calls=%fused_computation.7 | convolution fusion | flops 910098432 | bytes 4632576 | tf_op jit(solution)/shard_map/vmap(vmap())/dot_general | solution.py:57
  86.6 11.2 %while.1 = (s32[]{:T(128)}, f32[4,1,384,384]{3,2,1,0:T(8,128)}, s32[3,2]{0,1:T(2,128)S(1)}, f32[3,4,1,128,128]{4,3,0,2,1:T(8,128)}, s32[]{:T(128)}) while((s32[]{:T(128)}, f32[4,1,384,384]{3,2,1,0:T(8,128)}, s32[3,2]{0,1:T(2,128)S(1)}, f32[3,4,1,128,128]{4,3,0,2,1:T(8,128)}, s32[]{:T(128)}) %tuple.56), condition=%wide.while_cond, body=%wide.while_body.sunk | while | flops 2 | bytes 525421 | solution.py:63
  86.7 0.6 fusion.144
  87.3 3.1 bitcast_dynamic-update-slice_fusion.2
  91.0 3.1 bitcast_dynamic-update-slice_fusion.2
  94.8 3.0 bitcast_dynamic-update-slice_fusion.2
  97.8 118.9 %custom-call.4 = f32[4,1,3,128,128]{3,4,2,1,0:T(8,128)S(1)} custom-call(f32[4,1,3,128,128]{4,3,2,1,0:T(8,128)} %bitcast.622), custom_call_target="InvertDiagBlocksLowerTriangular" | custom-call | tf_op jit(solution)/shard_map/vmap(vmap(jit(_solve_triangular)))/triangular_solve | solution.py:63
  216.7 0.9 fusion.11
  217.6 0.6 fusion.34
  218.3 1.4 fusion.13
  219.7 0.6 convolution_bitcast_fusion.2
  220.3 1.7 fusion.15
  222.0 0.6 convolution_bitcast_fusion
  223.0 0.7 convolution_multiply_fusion.2
  223.7 1.1 convolution_multiply_fusion.1
  224.8 1.0 multiply_reduce_fusion.2
  225.8 0.8 fusion.36
  226.6 2.1 copy.202
  228.7 5.1 %all-to-all-start = ((bf16[128,16,128]{0,2,1:T(8,128)(2,1)}), bf16[128,16,128]{0,2,1:T(8,128)(2,1)S(1)}, u32[]{:S(2)}, u32[]{:S(2)}) async-start(bf16[128,16,128]{0,2,1:T(8,128)(2,1)} %bitcast.33), calls=%async_computation | async-start | bytes 1048576 | tf_op jit(solution)/shard_map/all_to_all | solution.py:154
  233.9 19.0 %all-to-all-done = bf16[128,16,128]{0,2,1:T(8,128)(2,1)S(1)} async-done(((bf16[128,16,128]{0,2,1:T(8,128)(2,1)}), bf16[128,16,128]{0,2,1:T(8,128)(2,1)S(1)}, u32[]{:S(2)}, u32[]{:S(2)}) %all-to-all-start) | async-done | bytes 524320 | tf_op jit(solution)/shard_map/all_to_all | solution.py:154
  253.1 20.5 %all-gather.13.cloned.1.call-done = bf16[512,2048]{1,0:T(8,128)(2,1)} async-done(((bf16[512,128]{1,0:T(8,128)(2,1)}), bf16[512,2048]{1,0:T(8,128)(2,1)}) %all-gather.13.cloned.1.call-update) | async-done | bytes 2097168 | tf_op jit(solution)/shard_map/all_gather | solution.py:156
  273.6 2.3 fusion.18
  276.0 0.6 gather_fusion
  276.6 0.9 stack.3
  277.6 15.5 %all-to-all-start.1 = ((bf16[512,1,4,128]{3,2,1,0:T(4,128)(2,1)}), bf16[512,1,4,128]{3,2,1,0:T(4,128)(2,1)S(1)}, u32[]{:S(2)}, u32[]{:S(2)}) async-start(bf16[512,1,4,128]{3,2,1,0:T(4,128)(2,1)} %stack.3), calls=%async_computation.1 | async-start | bytes 1048576 | tf_op jit(solution)/shard_map/all_to_all | solution.py:169
  293.7 2.1 fusion.17
  295.9 19.9 %all-to-all-done.1 = bf16[512,1,4,128]{3,2,1,0:T(4,128)(2,1)S(1)} async-done(((bf16[512,1,4,128]{3,2,1,0:T(4,128)(2,1)}), bf16[512,1,4,128]{3,2,1,0:T(4,128)(2,1)S(1)}, u32[]{:S(2)}, u32[]{:S(2)}) %all-to-all-start.1) | async-done | bytes 524320 | tf_op jit(solution)/shard_map/all_to_all | solution.py:169
  317.3 15.6 %all-gather.4 = f32[8,3,128]{2,1,0:T(4,128)S(1)} all-gather(f32[1,3,128]{2,1,0:T(4,128)S(1)} %maximum_bitcast_fusion.5), channel_id=2, replica_groups=mesh['batch_0'=8,'batch_1'=4,'head_0'=8,'head_1'=2] {'batch_0'}, dimensions={0}, use_global_device_ids=true | all-gather | bytes 13824 | tf_op jit(solution)/shard_map/all_gather | solution.py:26
  333.0 8.1 %all-gather.5 = f32[4,3,128]{2,1,0:T(4,128)S(1)} all-gather(f32[1,3,128]{2,1,0:T(4,128)S(1)} %maximum_bitcast_fusion.6), channel_id=3, replica_groups=mesh['batch_0'=8,'batch_1'=4,'head_0'=8,'head_1'=2] {'batch_1'}, dimensions={0}, use_global_device_ids=true | all-gather | bytes 7680 | tf_op jit(solution)/shard_map/all_gather | solution.py:26
  341.2 15.6 %all-gather.6 = f32[8,3,128]{2,1,0:T(4,128)S(1)} all-gather(f32[1,3,128]{2,1,0:T(4,128)S(1)} %maximum_bitcast_fusion.7), channel_id=4, replica_groups=mesh['batch_0'=8,'batch_1'=4,'head_0'=8,'head_1'=2] {'head_0'}, dimensions={0}, use_global_device_ids=true | all-gather | bytes 13824 | tf_op jit(solution)/shard_map/all_gather | solution.py:26
  356.8 14.8 %all-gather.7 = f32[2,3,128]{2,1,0:T(4,128)S(1)} all-gather(f32[1,3,128]{2,1,0:T(4,128)S(1)} %maximum_bitcast_fusion.8), channel_id=5, replica_groups=mesh['batch_0'=8,'batch_1'=4,'head_0'=8,'head_1'=2] {'head_1'}, dimensions={0}, use_global_device_ids=true | all-gather | bytes 4608 | tf_op jit(solution)/shard_map/all_gather | solution.py:26
  (120 shorter events, 8.8 us)
Async XLA Ops:
  7.2 309.6 %copy-start = (bf16[32,2048]{1,0:T(8,128)(2,1)S(1)}, bf16[32,2048]{1,0:T(8,128)(2,1)}, u32[]{:S(2)}) copy-start(bf16[32,2048]{1,0:T(8,128)(2,1)} %param.22) | copy-start | bytes 393220
  7.2 54.0 %copy-start.20 = (bf16[2048,4]{0,1:T(4,128)(2,1)S(1)}, bf16[2048,4]{0,1:T(4,128)(2,1)}, u32[]{:S(2)}) copy-start(bf16[2048,4]{0,1:T(4,128)(2,1)} %param.17) | copy-start | bytes 49156
  7.2 54.0 %copy-start.21 = (f32[2048]{0:T(1024)S(1)}, f32[2048]{0:T(1024)}, u32[]{:S(2)}) copy-start(f32[2048]{0:T(1024)} %param.15) | copy-start | bytes 24580
  7.2 51.9 %all-gather.11.cloned.1.call-start = ((), (), s32[]{:S(2)}) async-start(), calls=%async_computation.2 | async-start | bytes 2228224 | tf_op jit(solution)/shard_map/all_gather | solution.py:135
  7.9 265.7 %all-gather.13.cloned.1.call-start = ((), (), s32[]{:S(2)}) async-start(), calls=%async_computation.3 | async-start | bytes 2228224 | tf_op jit(solution)/shard_map/all_gather | solution.py:156
  13.2 50.4 %copy-start.17 = (s32[4]{0:T(128)S(1)}, s32[4]{0:T(128)}, u32[]{:S(2)}) copy-start(s32[4]{0:T(128)} %param.13) | copy-start | bytes 52
  61.2 5.0 %copy-start.1 = (bf16[512,2048]{1,0:T(8,128)(2,1)S(1)}, bf16[512,2048]{1,0:T(8,128)(2,1)}, u32[]{:S(2)}) copy-start(bf16[512,2048]{1,0:T(8,128)(2,1)} %all-gather.11.cloned.1.call-done) | copy-start | bytes 6291460
  63.6 13.1 %copy-start.9 = (f32[4,128,1,4]{1,0,3,2:T(4,128)}, f32[4,128,1,4]{1,0,3,2:T(4,128)S(1)}, u32[]{:S(2)}) copy-start(f32[4,128,1,4]{1,0,3,2:T(4,128)S(1)} %reshape.1819) | copy-start | bytes 24580
  78.6 0.9 slice-start
  78.6 1.1 copy-start.16
  78.9 2.4 copy-start.6
  79.0 2.3 copy-start.7
  80.8 0.5 copy-start.13
  81.3 5.3 %copy-start.10 = (f32[4,384]{1,0:T(4,128)}, f32[4,384]{1,0:T(4,128)S(1)}, u32[]{:S(2)}) copy-start(f32[4,384]{1,0:T(4,128)S(1)} %get-tuple-element.79) | copy-start | bytes 18436
  81.3 5.3 %copy-start.22 = (s32[3]{0:T(128)S(1)}, s32[3]{0:T(128)}, u32[]{:S(2)}) copy-start(s32[3]{0:T(128)} %iota_multiply_fusion) | copy-start | bytes 40
  86.6 130.1 %copy-start.2 = (f32[4,1,128,128]{3,2,1,0:T(8,128)S(1)}, f32[4,1,128,128]{3,2,1,0:T(8,128)}, u32[]{:S(2)}) copy-start(f32[4,1,128,128]{3,2,1,0:T(8,128)} %param.14) | copy-start | bytes 786436
  218.2 4.7 %copy-start.4 = (f32[4,128,1,1,128]{4,3,1,0,2:T(1,128)S(1)}, f32[4,128,1,1,128]{4,3,1,0,2:T(1,128)}, u32[]{:S(2)}) copy-start(f32[4,128,1,1,128]{4,3,1,0,2:T(1,128)} %slice.495) | copy-start | bytes 786436
  219.7 4.0 %copy-start.8 = (pred[128,384]{1,0:T(8,128)(4,1)S(1)}, pred[128,384]{1,0:T(8,128)(4,1)}, u32[]{:S(2)}) copy-start(pred[128,384]{1,0:T(8,128)(4,1)} %iota_compare_fusion.4) | copy-start | bytes 147460
  219.7 4.0 %copy-start.11 = (f32[4,384]{1,0:T(4,128)S(1)}, f32[4,384]{1,0:T(4,128)}, u32[]{:S(2)}) copy-start(f32[4,384]{1,0:T(4,128)} %copy-done.10) | copy-start | bytes 18436
  223.7 2.1 copy-start.15
  224.8 9.0 %copy-start.18 = (s32[4]{0:T(128)S(1)}, s32[4]{0:T(128)}, u32[]{:S(2)}) copy-start(s32[4]{0:T(128)} %param.13) | copy-start | bytes 52
  225.8 47.9 %copy-start.3 = (bf16[512,128]{1,0:T(8,128)(2,1)S(1)}, bf16[512,128]{1,0:T(8,128)(2,1)}, u32[]{:S(2)}) copy-start(bf16[512,128]{1,0:T(8,128)(2,1)} %param.12) | copy-start | bytes 393220
  228.7 24.2 %all-to-all-start = ((bf16[128,16,128]{0,2,1:T(8,128)(2,1)}), bf16[128,16,128]{0,2,1:T(8,128)(2,1)S(1)}, u32[]{:S(2)}, u32[]{:S(2)}) async-start(bf16[128,16,128]{0,2,1:T(8,128)(2,1)} %bitcast.33), calls=%async_computation | async-start | bytes 1048576 | tf_op jit(solution)/shard_map/all_to_all | solution.py:154
  253.1 39.9 %copy-start.14 = (f32[4]{0:T(128)S(1)}, f32[4]{0:T(128)}, u32[]{:S(2)}) copy-start(f32[4]{0:T(128)} %copy-done.13) | copy-start | bytes 52
  275.9 19.9 %copy-start.5 = (bf16[512,128]{1,0:T(8,128)(2,1)}, bf16[512,128]{1,0:T(8,128)(2,1)S(1)}, u32[]{:S(2)}) copy-start(bf16[512,128]{1,0:T(8,128)(2,1)S(1)} %fusion.18) | copy-start | bytes 393220
  277.6 38.2 %all-to-all-start.1 = ((bf16[512,1,4,128]{3,2,1,0:T(4,128)(2,1)}), bf16[512,1,4,128]{3,2,1,0:T(4,128)(2,1)S(1)}, u32[]{:S(2)}, u32[]{:S(2)}) async-start(bf16[512,1,4,128]{3,2,1,0:T(4,128)(2,1)} %stack.3), calls=%async_computation.1 | async-start | bytes 1048576 | tf_op jit(solution)/shard_map/all_to_all | solution.py:169
  295.9 20.9 %copy-start.12 = (f32[2048]{0:T(1024)S(1)}, f32[2048]{0:T(1024)}, u32[]{:S(2)}) copy-start(f32[2048]{0:T(1024)} %param.21) | copy-start | bytes 24580
  315.8 1.4 copy-start.19
Sparse Core Ops, SparseCore 0:
  10.1 48.9 all-gather.10
  226.7 46.8 all-gather.12
